TPU v7x, 32 devices: a whole 2x2x4 slice. The times are simulated.
32 devices in a mesh: dom: 16 (over z, y, x), col: 2 (over core).
Axes of the slice: x: 2, y: 2, z: 4, core: 2. Of those that a mesh axis runs over, the one named last changes fastest.
Arguments:
- features: bfloat16 [16384, 256], P(('dom', 'col')), may hold values from -6 to 6
- weight: bfloat16 [256, 256], replicated, may hold values from -0.375 to 0.375
- cotangent: bfloat16 [16384, 256], P(('dom', 'col')), may hold values from -6 to 6
- tile_values: bfloat16 [1280, 128, 128], P(('dom', 'col')), may hold values from -0.15625 to 0.15625
- tile_rows: int32 [1280], P(('dom', 'col')), may hold values from 0 to 7
- tile_cols: int32 [1280], P(('dom', 'col')), may hold values from 0 to 19, as said below
- tile_count: int32 [32], P(('dom', 'col')), may hold values from 20 to 40, as said below
- send_blocks: int32 [32, 16], P(('dom', 'col')), may hold values from 0 to 3
Outputs:
- output_rows: bfloat16 [16384, 256], P(('dom', 'col'))
- feature_grad: bfloat16 [16384, 256], P(('dom', 'col'))
- weight_grad: float32 [256, 256], replicated
Inputs may be any that keep to these rules, and one draw needn't show every extreme that they name: `tile_cols`: A value v below 4 names the device's own row block v; a value 4 + s names the row block that the device of partition s with the same col index sends to this partition; no receive slot is named by two tiles of one device. Only the first tile_count slots of a device's tiles are live; some device has all 40 live.
All inputs are finite; a program needn't handle non-finite values.
Results may differ from a plain program's by a relative error of at most 0.0049.
Values may be sent and summed in bfloat16 or wider, within the bound.
A program may use at most 128 MiB of HBM per device.

v0:
```python
import jax
import jax.numpy as jnp
from jax import lax
from jax.sharding import PartitionSpec as P


def local(features, weight, cotangent, tile_values, tile_rows, tile_cols, tile_count, send_blocks):
    block_size = tile_values.shape[1]
    half_blocks = features.shape[0] // block_size
    width_in = features.shape[1]
    peer_count = send_blocks.shape[1]
    all_blocks = half_blocks * lax.axis_size("col")
    node_total = features.shape[0] * lax.axis_size("col") * lax.axis_size("dom")
    own_blocks = features.reshape(half_blocks, block_size, width_in)
    outgoing = own_blocks[send_blocks[0]]
    incoming = lax.all_to_all(outgoing, "dom", split_axis=0, concat_axis=0, tiled=True)
    sources = jnp.concatenate([own_blocks, incoming], axis=0)
    live_bool = jnp.arange(tile_values.shape[0], dtype=jnp.int32) < tile_count[0]
    live_mask = live_bool.astype(jnp.bfloat16)
    masked_tiles = tile_values * live_mask[:, None, None]
    picked = sources[tile_cols]
    products = jnp.einsum("tij,tjf->tif", masked_tiles, picked, preferred_element_type=jnp.float32)
    partial_value = jax.ops.segment_sum(products, tile_rows, num_segments=all_blocks)
    summed = lax.psum_scatter(partial_value, "col", scatter_dimension=0, tiled=True)
    hidden = summed.astype(jnp.bfloat16).reshape(half_blocks * block_size, width_in)
    output_rows = jnp.dot(hidden, weight, preferred_element_type=jnp.float32).astype(jnp.bfloat16)
    own_grad = lax.dot_general(
        cotangent, weight, (((1,), (1,)), ((), ())), preferred_element_type=jnp.float32
    ).astype(jnp.bfloat16)
    own_grad = own_grad.reshape(half_blocks, block_size, width_in)
    grad_blocks = lax.all_gather(own_grad, "col", axis=0, tiled=True)
    chosen = grad_blocks[tile_rows]
    back_terms = jnp.einsum(
        "tji,tjf->tif", masked_tiles, chosen, preferred_element_type=jnp.float32
    )
    spread = jax.ops.segment_sum(back_terms, tile_cols, num_segments=half_blocks + peer_count)
    returned = lax.all_to_all(spread[half_blocks:], "dom", split_axis=0, concat_axis=0, tiled=True)
    grad_total = spread[:half_blocks] + jax.ops.segment_sum(
        returned, send_blocks[0], num_segments=half_blocks
    )
    feature_grad = grad_total.astype(jnp.bfloat16).reshape(half_blocks * block_size, width_in)
    local_weight = lax.dot_general(
        hidden, cotangent, (((0,), (0,)), ((), ())), preferred_element_type=jnp.float32
    )
    local_weight = local_weight * jnp.float32(1.0 / node_total**0.5)
    col_share = lax.psum_scatter(local_weight, "col", scatter_dimension=0, tiled=True)
    dom_share = lax.psum(col_share, "dom")
    weight_grad = lax.all_gather(dom_share, "col", axis=0, tiled=True)
    return (output_rows, feature_grad, weight_grad)


def solution(mesh):
    return jax.shard_map(
        local,
        mesh=mesh,
        in_specs=(
            P(("dom", "col"), None),
            P(),
            P(("dom", "col"), None),
            P(("dom", "col"), None, None),
            P(("dom", "col")),
            P(("dom", "col")),
            P(("dom", "col")),
            P(("dom", "col"), None),
        ),
        out_specs=(P(("dom", "col"), None), P(("dom", "col"), None), P()),
        check_vma=False,
    )
```

profile of v0, /device:TPU:0, one launch (start us, length us, event | category | flops | bytes accessed | tf_op | source)
XLA Modules:
  0.0 214.5 jit_solution(6143368337666922137)
XLA Ops:
  7.2 0.0 copy-start
  7.2 0.0 copy-start.7
  7.2 0.0 copy-start.5
  7.2 0.7 fusion.6
  7.9 2.6 %gather_fusion = bf16[16,128,256]{2,1,0:T(8,128)(2,1)} fusion(bf16[4,128,256]{2,1,0:T(8,128)(2,1)} %bitcast.19, s32[1024]{0:T(1024)S(1)} %pad_clamp_fusion.2), kind=kCustom, calls=%fused_computation | custom fusion | bytes 2097216 | tf_op jit(solution)/shard_map/gather | solution.py:15
  10.5 8.4 %all-to-all-start = ((bf16[16,128,256]{2,1,0:T(8,128)(2,1)}), bf16[16,128,256]{2,1,0:T(8,128)(2,1)}, u32[]{:S(2)}, u32[]{:S(2)}) async-start(bf16[16,128,256]{2,1,0:T(8,128)(2,1)} %gather_fusion), calls=%async_computation | async-start | bytes 2097152 | tf_op jit(solution)/shard_map/all_to_all | solution.py:16
  19.5 0.0 copy-done.7
  19.6 0.0 copy-done
  19.6 0.0 copy-done.5
  19.6 0.3 convolution_convert_fusion
  19.9 2.2 %all_gather.6 = bf16[8,128,256]{2,1,0:T(8,128)(2,1)S(1)} all-gather(bf16[4,128,256]{2,1,0:T(8,128)(2,1)S(1)} %bitcast.23), channel_id=1, replica_groups=mesh['dom'=16,'col'=2] {'col'}, dimensions={0}, use_global_device_ids=true | all-gather | bytes 786432 | tf_op jit(solution)/shard_map/all_gather | solution.py:31
  22.0 0.7 gather_fusion.2
  22.8 4.9 %fusion = f32[40,128,256]{2,1,0:T(8,128)} fusion(bf16[40,128,256]{2,1,0:T(8,128)(2,1)S(1)} %gather_fusion.2, bf16[40,128,128]{2,1,0:T(8,128)(2,1)} %param.11, bf16[40]{0:T(256)(128)(2,1)S(1)} %compare_convert_fusion), kind=kOutput, calls=%fused_computation.10 | convolution fusion | flops 336199680 | bytes 9175120 | tf_op jit(solution)/shard_map/tji,tjf->tif/dot_general | solution.py:33
  27.7 0.0 copy-start.6
  27.7 0.3 broadcast_in_dim.24
  28.0 0.4 copy-done.6
  28.4 9.1 %scatter_fusion.1 = f32[20,128,256]{2,1,0:T(8,128)S(1)} fusion(f32[20,128,256]{2,1,0:T(8,128)S(1)} %broadcast_in_dim.24, s32[40]{0:T(128)S(1)} %copy-done.6, f32[40,128,256]{2,1,0:T(8,128)} %fusion), kind=kCustom, calls=%fused_computation.4 | custom fusion | flops 1310720 | bytes 15728800 | tf_op jit(solution)/shard_map/scatter-add | solution.py:36
  37.4 0.0 copy-start.2
  37.4 1.8 slice.15
  39.2 0.0 copy-start.3
  39.2 4.1 %all-to-all-done = bf16[16,128,256]{2,1,0:T(8,128)(2,1)} async-done(((bf16[16,128,256]{2,1,0:T(8,128)(2,1)}), bf16[16,128,256]{2,1,0:T(8,128)(2,1)}, u32[]{:S(2)}, u32[]{:S(2)}) %all-to-all-start) | async-done | bytes 1048608 | tf_op jit(solution)/shard_map/all_to_all | solution.py:16
  43.3 0.0 copy-done.2
  43.3 5.9 %all-to-all-start.1 = ((f32[16,128,256]{2,1,0:T(8,128)}), f32[16,128,256]{2,1,0:T(8,128)}, u32[]{:S(2)}, u32[]{:S(2)}) async-start(f32[16,128,256]{2,1,0:T(8,128)} %slice.15), calls=%async_computation.2 | async-start | bytes 4194304 | tf_op jit(solution)/shard_map/all_to_all | solution.py:37
  49.3 0.0 reduce-scatter.3.cloned.1.call-start
  49.3 0.0 copy-done.3
  49.4 1.3 pad_maximum_fusion
  50.7 0.0 copy-start.4
  50.7 2.4 %gather_fusion.1 = bf16[40,128,256]{2,1,0:T(8,128)(2,1)} fusion(bf16[20,128,256]{2,1,0:T(8,128)(2,1)S(1)} %pad_maximum_fusion, s32[1024]{0:T(1024)S(1)} %pad_clamp_fusion.1), kind=kCustom, calls=%fused_computation.1 | custom fusion | bytes 5243040 | tf_op jit(solution)/shard_map/gather | solution.py:21
  53.1 0.0 copy-done.4
  53.1 4.9 %fusion.2 = f32[40,128,256]{2,1,0:T(8,128)} fusion(bf16[40,128,256]{2,1,0:T(8,128)(2,1)} %gather_fusion.1, bf16[40,128,128]{2,1,0:T(8,128)(2,1)S(1)} %copy-done.4, bf16[40]{0:T(256)(128)(2,1)S(1)} %compare_convert_fusion), kind=kOutput, calls=%fused_computation.12 | convolution fusion | flops 336199680 | bytes 9175120 | tf_op jit(solution)/shard_map/tij,tjf->tif/dot_general | solution.py:22
  58.1 0.1 broadcast_in_dim.21
  58.1 9.0 %scatter_fusion = f32[8,128,256]{2,1,0:T(8,128)S(1)} fusion(f32[8,128,256]{2,1,0:T(8,128)S(1)} %broadcast_in_dim.21, s32[40]{0:T(128)S(1)} %copy-done.7, f32[40,128,256]{2,1,0:T(8,128)} %fusion.2), kind=kCustom, calls=%fused_computation.3 | custom fusion | flops 1310720 | bytes 15728800 | tf_op jit(solution)/shard_map/scatter-add | solution.py:23
  67.2 0.0 copy-start.1
  67.2 0.0 copy-start.8
  67.2 1.1 copy-done.1
  68.3 0.0 reduce-scatter.3.cloned.1.call-update
  68.3 0.0 reduce-scatter.5.cloned.1.call-start
  68.4 9.7 %reduce-scatter.3.cloned.1.call-done = f32[4,128,256]{2,1,0:T(8,128)} async-done(((f32[8,128,256]{2,1,0:T(8,128)}), f32[4,128,256]{2,1,0:T(8,128)}) %reduce-scatter.3.cloned.1.call-update) | async-done | bytes 524304 | tf_op jit(solution)/shard_map/reduce_scatter | solution.py:24
  78.1 1.1 convert_element_type.20
  79.1 1.0 convolution_multiply_fusion
  80.1 0.0 reduce-scatter.5.cloned.1.call-update
  80.1 0.0 all-reduce.2.cloned.1.call-start
  80.2 1.1 slice.14
  81.3 10.0 %all-to-all-done.1 = f32[16,128,256]{2,1,0:T(8,128)} async-done(((f32[16,128,256]{2,1,0:T(8,128)}), f32[16,128,256]{2,1,0:T(8,128)}, u32[]{:S(2)}, u32[]{:S(2)}) %all-to-all-start.1) | async-done | bytes 2097184 | tf_op jit(solution)/shard_map/all_to_all | solution.py:37
  91.2 0.0 copy-done.8
  91.2 3.5 %scatter_fusion.2 = f32[4,128,256]{2,1,0:T(8,128)S(1)} fusion(f32[4,128,256]{2,1,0:T(8,128)S(1)} %slice.14, s32[16]{0:T(128)S(1)} %bitcast.25, f32[16,128,256]{2,1,0:T(8,128)} %all-to-all-done.1), kind=kCustom, calls=%fused_computation.5 | custom fusion | flops 524288 | bytes 6291520 | tf_op jit(solution)/shard_map/scatter-add | solution.py:38
  94.7 0.7 convert_element_type.23
  95.4 0.0 reduce-scatter.5.cloned.1.call-done
  95.4 0.0 all-reduce.2.cloned.1.call-update
  95.5 0.9 convolution_convert_fusion.1
  96.4 108.7 %all-reduce.2.cloned.1.call-done = f32[128,256]{1,0:T(8,128)} async-done(((f32[128,256]{1,0:T(8,128)}), f32[128,256]{1,0:T(8,128)}) %all-reduce.2.cloned.1.call-update) | async-done | bytes 131088 | tf_op jit(solution)/shard_map/psum | solution.py:47
  205.1 2.2 %all_gather.7 = f32[256,256]{1,0:T(8,128)S(1)} all-gather(f32[128,256]{1,0:T(8,128)} %all-reduce.2.cloned.1.call-done), channel_id=1, replica_groups=mesh['dom'=16,'col'=2] {'col'}, dimensions={0}, use_global_device_ids=true | all-gather | bytes 393216 | tf_op jit(solution)/shard_map/all_gather | solution.py:48
  207.3 0.7 copy.20
  (6 shorter events, 0.0 us)
Async XLA Ops:
  7.2 12.4 %copy-start = (bf16[512,256]{1,0:T(8,128)(2,1)S(1)}, bf16[512,256]{1,0:T(8,128)(2,1)}, u32[]{:S(2)}) copy-start(bf16[512,256]{1,0:T(8,128)(2,1)} %param.10) | copy-start | bytes 786436
  7.2 12.4 %copy-start.7 = (s32[40]{0:T(128)S(1)}, s32[40]{0:T(128)}, u32[]{:S(2)}) copy-start(s32[40]{0:T(128)} %param.12) | copy-start | bytes 484
  7.2 12.4 %copy-start.5 = (bf16[256,256]{1,0:T(8,128)(2,1)S(1)}, bf16[256,256]{1,0:T(8,128)(2,1)}, u32[]{:S(2)}) copy-start(bf16[256,256]{1,0:T(8,128)(2,1)} %param.9) | copy-start | bytes 393220
  10.5 32.8 %all-to-all-start = ((bf16[16,128,256]{2,1,0:T(8,128)(2,1)}), bf16[16,128,256]{2,1,0:T(8,128)(2,1)}, u32[]{:S(2)}, u32[]{:S(2)}) async-start(bf16[16,128,256]{2,1,0:T(8,128)(2,1)} %gather_fusion), calls=%async_computation | async-start | bytes 2097152 | tf_op jit(solution)/shard_map/all_to_all | solution.py:16
  27.7 0.7 copy-start.6
  37.4 5.9 %copy-start.2 = (f32[20,128,256]{2,1,0:T(8,128)}, f32[20,128,256]{2,1,0:T(8,128)S(1)}, u32[]{:S(2)}) copy-start(f32[20,128,256]{2,1,0:T(8,128)S(1)} %scatter_fusion.1) | copy-start | bytes 7864324
  39.2 10.1 %copy-start.3 = (bf16[512,256]{1,0:T(8,128)(2,1)S(1)}, bf16[512,256]{1,0:T(8,128)(2,1)}, u32[]{:S(2)}) copy-start(bf16[512,256]{1,0:T(8,128)(2,1)} %param.8) | copy-start | bytes 786436
  43.3 47.9 %all-to-all-start.1 = ((f32[16,128,256]{2,1,0:T(8,128)}), f32[16,128,256]{2,1,0:T(8,128)}, u32[]{:S(2)}, u32[]{:S(2)}) async-start(f32[16,128,256]{2,1,0:T(8,128)} %slice.15), calls=%async_computation.2 | async-start | bytes 4194304 | tf_op jit(solution)/shard_map/all_to_all | solution.py:37
  49.3 28.8 %reduce-scatter.3.cloned.1.call-start = ((), (), s32[]{:S(2)}) async-start(), calls=%async_computation.4 | async-start | bytes 1572864 | tf_op jit(solution)/shard_map/reduce_scatter | solution.py:24
  50.7 2.4 %copy-start.4 = (bf16[40,128,128]{2,1,0:T(8,128)(2,1)S(1)}, bf16[40,128,128]{2,1,0:T(8,128)(2,1)}, u32[]{:S(2)}) copy-start(bf16[40,128,128]{2,1,0:T(8,128)(2,1)} %param.11) | copy-start | bytes 3932164
  67.2 1.1 copy-start.1
  67.2 24.0 %copy-start.8 = (s32[1,16]{1,0:T(1,128)S(1)}, s32[1,16]{1,0:T(1,128)}, u32[]{:S(2)}) copy-start(s32[1,16]{1,0:T(1,128)} %param.15) | copy-start | bytes 196
  68.3 27.1 %reduce-scatter.5.cloned.1.call-start = ((), (), s32[]{:S(2)}) async-start(), calls=%async_computation.5 | async-start | bytes 393216 | tf_op jit(solution)/shard_map/reduce_scatter | solution.py:46
  80.1 125.0 %all-reduce.2.cloned.1.call-start = ((), (), s32[]{:S(2)}) async-start(), calls=%async_computation.6 | async-start | bytes 262144 | tf_op jit(solution)/shard_map/psum | solution.py:47
Sparse Core Ops, SparseCore 0:
  68.4 9.5 reduce-scatter.2
  80.9 8.9 reduce-scatter.4
  95.6 109.4 all-reduce.1
where the time goes:
time: 215 us
  waiting for transfers between devices  133 us (62%)
  other arithmetic  25.5 us (12%)
  between operations  14.6 us (7%)
  starting transfers between devices  14.4 us (7%)
  matrix products  12 us (6%)
  local copies, waits for them, and re-layouts  11.1 us (5%)
  blocking collectives  4.37 us (2%)
    psum x1, waiting for transfers between devices, local(): dom_share = lax.psum(col_share, 'dom')  109 us
    all_to_all x1, waiting for transfers between devices, local(): lax.all_to_all(spread[half_blocks:], 'dom', split_axis=0, concat_axis=0,...  9.95 us
    reduce_scatter x1, waiting for transfers between devices, local(): lax.psum_scatter(partial_value, 'col', scatter_dimension=0, tiled=True)  9.71 us
    scatter-add x1, other arithmetic, local(): jax.ops.segment_sum(back_terms, tile_cols, num_segments=half_blocks + pee...  9.08 us
    scatter-add x1, other arithmetic, local(): jax.ops.segment_sum(products, tile_rows, num_segments=all_blocks)  9.04 us
    all_to_all x1, starting transfers between devices, local(): lax.all_to_all(outgoing, 'dom', split_axis=0, concat_axis=0, tiled=True)  8.39 us
    all_to_all x1, starting transfers between devices, local(): lax.all_to_all(spread[half_blocks:], 'dom', split_axis=0, concat_axis=0,...  5.93 us
    dot_general x1, matrix products, local(): jnp.einsum('tij,tjf->tif', masked_tiles, picked, preferred_element_type=j...  4.93 us
  transfers between devices with their start and end apart: 5, of which 4 were waited for; matrix products, arithmetic and copies ran while one was open for 20% of the time, Pallas kernels for 0%

commit v1 on v0

--- a/solution.py
+++ b/solution.py
@@ -44,7 +44,8 @@
     )
     local_weight = local_weight * jnp.float32(1.0 / node_total**0.5)
     col_share = lax.psum_scatter(local_weight, "col", scatter_dimension=0, tiled=True)
-    dom_share = lax.psum(col_share, "dom")
+    pieces = lax.all_gather(col_share, "dom", axis=0, tiled=False)
+    dom_share = pieces.sum(axis=0)
     weight_grad = lax.all_gather(dom_share, "col", axis=0, tiled=True)
     return (output_rows, feature_grad, weight_grad)
 

time: 215 us -> 185 us (0.86)
  waiting for transfers between devices: 133 us -> 102 us
    psum x1 -> x0, waiting for transfers between devices: 109 us -> none  [local(): dom_share = lax.psum(col_share, 'dom')]
    all_to_all x1, waiting for transfers between devices: 9.95 us -> 48.3 us  [local(): lax.all_to_all(spread[half_blocks:], 'dom', split_axis=0, concat_axis=0,...]
    all_gather x0 -> x1, waiting for transfers between devices: none -> 24.1 us  [local(): pieces = lax.all_gather(col_share, 'dom', axis=0, tiled=False)]
    all_to_all x1, waiting for transfers between devices: 4.13 us -> 23.6 us  [local(): lax.all_to_all(outgoing, 'dom', split_axis=0, concat_axis=0, tiled=True)]
    reduce_scatter x1, waiting for transfers between devices: 9.71 us -> 5.54 us  [local(): lax.psum_scatter(partial_value, 'col', scatter_dimension=0, tiled=True)]
  transfers between devices with their start and end apart: 5 -> 5, of which waited for: 4 -> 4; matrix products, arithmetic and copies ran while one was open for 20% -> 12% of each run, Pallas kernels for 0% -> 0%
where the time goes in v1:
time: 185 us
  waiting for transfers between devices  102 us (55%)
  other arithmetic  26 us (14%)
  starting transfers between devices  15.5 us (8%)
  between operations  14.6 us (8%)
  matrix products  12 us (6%)
  local copies, waits for them, and re-layouts  9.94 us (5%)
  blocking collectives  4.18 us (2%)
    all_to_all x1, waiting for transfers between devices, local(): lax.all_to_all(spread[half_blocks:], 'dom', split_axis=0, concat_axis=0,...  48.3 us
    all_gather x1, waiting for transfers between devices, local(): pieces = lax.all_gather(col_share, 'dom', axis=0, tiled=False)  24.1 us
    all_to_all x1, waiting for transfers between devices, local(): lax.all_to_all(outgoing, 'dom', split_axis=0, concat_axis=0, tiled=True)  23.6 us
    scatter-add x1, other arithmetic, local(): jax.ops.segment_sum(back_terms, tile_cols, num_segments=half_blocks + pee...  9.1 us
    scatter-add x1, other arithmetic, local(): jax.ops.segment_sum(products, tile_rows, num_segments=all_blocks)  9.04 us
    all_to_all x1, starting transfers between devices, local(): lax.all_to_all(outgoing, 'dom', split_axis=0, concat_axis=0, tiled=True)  8.34 us
    all_to_all x1, starting transfers between devices, local(): lax.all_to_all(spread[half_blocks:], 'dom', split_axis=0, concat_axis=0,...  7.02 us
    reduce_scatter x1, waiting for transfers between devices, local(): lax.psum_scatter(partial_value, 'col', scatter_dimension=0, tiled=True)  5.54 us
  transfers between devices with their start and end apart: 5, of which 4 were waited for; matrix products, arithmetic and copies ran while one was open for 12% of the time, Pallas kernels for 0%

profile of v1, /device:TPU:0, one launch (start us, length us, event | category | flops | bytes accessed | tf_op | source)
XLA Modules:
  0.0 184.6 jit_solution(2431246527061912870)
XLA Ops:
  7.2 0.0 copy-start
  7.2 0.0 copy-start.2
  7.2 0.0 copy-start.8
  7.2 0.7 fusion.6
  7.9 2.5 %gather_fusion = bf16[16,128,256]{2,1,0:T(8,128)(2,1)} fusion(bf16[4,128,256]{2,1,0:T(8,128)(2,1)} %bitcast.20, s32[1024]{0:T(1024)S(1)} %pad_clamp_fusion.2), kind=kCustom, calls=%fused_computation | custom fusion | bytes 2097216 | tf_op jit(solution)/shard_map/gather | solution.py:15
  10.5 8.3 %all-to-all-start = ((bf16[16,128,256]{2,1,0:T(8,128)(2,1)}), bf16[16,128,256]{2,1,0:T(8,128)(2,1)S(1)}, u32[]{:S(2)}, u32[]{:S(2)}) async-start(bf16[16,128,256]{2,1,0:T(8,128)(2,1)} %gather_fusion), calls=%async_computation | async-start | bytes 2097152 | tf_op jit(solution)/shard_map/all_to_all | solution.py:16
  18.8 0.0 reduce-scatter.3.cloned.1.call-start
  19.5 0.0 copy-done.8
  19.6 23.6 %all-to-all-done = bf16[16,128,256]{2,1,0:T(8,128)(2,1)S(1)} async-done(((bf16[16,128,256]{2,1,0:T(8,128)(2,1)}), bf16[16,128,256]{2,1,0:T(8,128)(2,1)S(1)}, u32[]{:S(2)}, u32[]{:S(2)}) %all-to-all-start) | async-done | bytes 1048608 | tf_op jit(solution)/shard_map/all_to_all | solution.py:16
  43.2 0.0 copy-done.2
  43.2 0.1 pad_maximum_fusion
  43.3 0.0 copy-start.3
  43.3 2.4 %gather_fusion.1 = bf16[40,128,256]{2,1,0:T(8,128)(2,1)} fusion(bf16[20,128,256]{2,1,0:T(8,128)(2,1)S(1)} %pad_maximum_fusion, s32[1024]{0:T(1024)S(1)} %pad_clamp_fusion.1), kind=kCustom, calls=%fused_computation.1 | custom fusion | bytes 5243040 | tf_op jit(solution)/shard_map/gather | solution.py:21
  45.7 0.0 copy-done.3
  45.7 0.0 copy-start.7
  45.7 4.9 %fusion.2 = f32[40,128,256]{2,1,0:T(8,128)} fusion(bf16[40,128,256]{2,1,0:T(8,128)(2,1)} %gather_fusion.1, bf16[40,128,128]{2,1,0:T(8,128)(2,1)S(1)} %copy-done.3, bf16[40]{0:T(256)(128)(2,1)S(1)} %compare_convert_fusion), kind=kOutput, calls=%fused_computation.12 | convolution fusion | flops 336199680 | bytes 9175120 | tf_op jit(solution)/shard_map/tij,tjf->tif/dot_general | solution.py:22
  50.6 0.1 broadcast_in_dim.21
  50.7 0.0 copy-done.7
  50.7 0.0 copy-start.6
  50.8 9.0 %scatter_fusion = f32[8,128,256]{2,1,0:T(8,128)S(1)} fusion(f32[8,128,256]{2,1,0:T(8,128)S(1)} %broadcast_in_dim.21, s32[40]{0:T(128)S(1)} %copy-done.7, f32[40,128,256]{2,1,0:T(8,128)} %fusion.2), kind=kCustom, calls=%fused_computation.3 | custom fusion | flops 1310720 | bytes 15728800 | tf_op jit(solution)/shard_map/scatter-add | solution.py:23
  59.8 0.0 copy-start.1
  59.8 1.0 copy-done.1
  60.8 0.0 reduce-scatter.3.cloned.1.call-update
  60.8 0.0 reduce-scatter.5.cloned.1.call-start
  60.9 0.0 copy-done
  60.9 0.0 copy-done.6
  60.9 0.3 convolution_convert_fusion
  61.2 2.2 %all_gather.12 = bf16[8,128,256]{2,1,0:T(8,128)(2,1)S(1)} all-gather(bf16[4,128,256]{2,1,0:T(8,128)(2,1)S(1)} %bitcast.25), channel_id=1, replica_groups=mesh['dom'=16,'col'=2] {'col'}, dimensions={0}, use_global_device_ids=true | all-gather | bytes 786432 | tf_op jit(solution)/shard_map/all_gather | solution.py:31
  63.3 0.7 gather_fusion.2
  64.1 5.5 %reduce-scatter.3.cloned.1.call-done = f32[4,128,256]{2,1,0:T(8,128)} async-done(((f32[8,128,256]{2,1,0:T(8,128)}), f32[4,128,256]{2,1,0:T(8,128)}) %reduce-scatter.3.cloned.1.call-update) | async-done | bytes 524304 | tf_op jit(solution)/shard_map/reduce_scatter | solution.py:24
  69.6 1.1 convert_element_type.20
  70.7 0.0 copy-start.4
  70.7 0.7 copy-done.4
  71.4 1.0 convolution_multiply_fusion
  72.4 0.0 reduce-scatter.5.cloned.1.call-update
  72.4 4.9 %fusion = f32[40,128,256]{2,1,0:T(8,128)} fusion(bf16[40,128,256]{2,1,0:T(8,128)(2,1)S(1)} %gather_fusion.2, bf16[40,128,128]{2,1,0:T(8,128)(2,1)} %param.11, bf16[40]{0:T(256)(128)(2,1)S(1)} %compare_convert_fusion), kind=kOutput, calls=%fused_computation.10 | convolution fusion | flops 336199680 | bytes 9175120 | tf_op jit(solution)/shard_map/tji,tjf->tif/dot_general | solution.py:33
  77.3 0.3 broadcast_in_dim.24
  77.6 9.1 %scatter_fusion.1 = f32[20,128,256]{2,1,0:T(8,128)S(1)} fusion(f32[20,128,256]{2,1,0:T(8,128)S(1)} %broadcast_in_dim.24, s32[40]{0:T(128)S(1)} %copy-done.8, f32[40,128,256]{2,1,0:T(8,128)} %fusion), kind=kCustom, calls=%fused_computation.4 | custom fusion | flops 1310720 | bytes 15728800 | tf_op jit(solution)/shard_map/scatter-add | solution.py:36
  86.7 1.5 slice.15
  88.2 0.0 copy-start.9
  88.2 7.0 %all-to-all-start.1 = ((f32[16,128,256]{2,1,0:T(8,128)}), f32[16,128,256]{2,1,0:T(8,128)}, u32[]{:S(2)}, u32[]{:S(2)}) async-start(f32[16,128,256]{2,1,0:T(8,128)} %slice.15), calls=%async_computation.2 | async-start | bytes 4194304 | tf_op jit(solution)/shard_map/all_to_all | solution.py:37
  95.3 0.0 all-gather.3.cloned.1.call-start
  95.3 0.0 reduce-scatter.5.cloned.1.call-done
  95.3 0.7 all-gather.3.cloned.1.call-update
  96.0 48.3 %all-to-all-done.1 = f32[16,128,256]{2,1,0:T(8,128)} async-done(((f32[16,128,256]{2,1,0:T(8,128)}), f32[16,128,256]{2,1,0:T(8,128)}, u32[]{:S(2)}, u32[]{:S(2)}) %all-to-all-start.1) | async-done | bytes 2097184 | tf_op jit(solution)/shard_map/all_to_all | solution.py:37
  144.3 0.0 copy-done.9
  144.3 0.0 copy-start.5
  144.3 3.5 %scatter_fusion.2 = f32[4,128,256]{2,1,0:T(8,128)S(1)} fusion(f32[4,128,256]{2,1,0:T(8,128)S(1)} %slice.14, s32[16]{0:T(128)S(1)} %bitcast.27, f32[16,128,256]{2,1,0:T(8,128)} %all-to-all-done.1), kind=kCustom, calls=%fused_computation.5 | custom fusion | flops 524288 | bytes 6291520 | tf_op jit(solution)/shard_map/scatter-add | solution.py:38
  147.8 0.7 convert_element_type.23
  148.6 0.0 copy-done.5
  148.6 0.9 convolution_convert_fusion.1
  149.5 24.1 %all-gather.3.cloned.1.call-done = f32[2048,256]{1,0:T(8,128)} async-done(((f32[128,256]{1,0:T(8,128)}), f32[2048,256]{1,0:T(8,128)}) %all-gather.3.cloned.1.call-update) | async-done | bytes 2097168 | tf_op jit(solution)/shard_map/all_gather | solution.py:47
  173.6 1.7 reduce_sum.9
  175.3 2.0 %all_gather.15 = f32[256,256]{1,0:T(8,128)S(1)} all-gather(f32[128,256]{1,0:T(8,128)S(1)} %reduce_sum.9), channel_id=1, replica_groups=mesh['dom'=16,'col'=2] {'col'}, dimensions={0}, use_global_device_ids=true | all-gather | bytes 393216 | tf_op jit(solution)/shard_map/all_gather | solution.py:49
  177.3 0.7 copy.19
  (7 shorter events, 0.1 us)
Async XLA Ops:
  7.2 53.7 %copy-start = (bf16[512,256]{1,0:T(8,128)(2,1)S(1)}, bf16[512,256]{1,0:T(8,128)(2,1)}, u32[]{:S(2)}) copy-start(bf16[512,256]{1,0:T(8,128)(2,1)} %param.10) | copy-start | bytes 786436
  7.2 36.0 %copy-start.2 = (bf16[512,256]{1,0:T(8,128)(2,1)S(1)}, bf16[512,256]{1,0:T(8,128)(2,1)}, u32[]{:S(2)}) copy-start(bf16[512,256]{1,0:T(8,128)(2,1)} %param.8) | copy-start | bytes 786436
  7.2 12.3 %copy-start.8 = (s32[40]{0:T(128)S(1)}, s32[40]{0:T(128)}, u32[]{:S(2)}) copy-start(s32[40]{0:T(128)} %param.13) | copy-start | bytes 484
  10.5 32.7 %all-to-all-start = ((bf16[16,128,256]{2,1,0:T(8,128)(2,1)}), bf16[16,128,256]{2,1,0:T(8,128)(2,1)S(1)}, u32[]{:S(2)}, u32[]{:S(2)}) async-start(bf16[16,128,256]{2,1,0:T(8,128)(2,1)} %gather_fusion), calls=%async_computation | async-start | bytes 2097152 | tf_op jit(solution)/shard_map/all_to_all | solution.py:16
  18.8 50.8 %reduce-scatter.3.cloned.1.call-start = ((), (), s32[]{:S(2)}) async-start(), calls=%async_computation.4 | async-start | bytes 1572864 | tf_op jit(solution)/shard_map/reduce_scatter | solution.py:24
  43.3 2.4 %copy-start.3 = (bf16[40,128,128]{2,1,0:T(8,128)(2,1)S(1)}, bf16[40,128,128]{2,1,0:T(8,128)(2,1)}, u32[]{:S(2)}) copy-start(bf16[40,128,128]{2,1,0:T(8,128)(2,1)} %param.11) | copy-start | bytes 3932164
  45.7 5.0 %copy-start.7 = (s32[40]{0:T(128)S(1)}, s32[40]{0:T(128)}, u32[]{:S(2)}) copy-start(s32[40]{0:T(128)} %param.12) | copy-start | bytes 484
  50.7 10.1 %copy-start.6 = (bf16[256,256]{1,0:T(8,128)(2,1)S(1)}, bf16[256,256]{1,0:T(8,128)(2,1)}, u32[]{:S(2)}) copy-start(bf16[256,256]{1,0:T(8,128)(2,1)} %param.9) | copy-start | bytes 393220
  59.8 1.0 copy-start.1
  60.8 34.5 %reduce-scatter.5.cloned.1.call-start = ((), (), s32[]{:S(2)}) async-start(), calls=%async_computation.5 | async-start | bytes 393216 | tf_op jit(solution)/shard_map/reduce_scatter | solution.py:46
  70.7 0.7 copy-start.4
  88.2 56.1 %copy-start.9 = (s32[1,16]{1,0:T(1,128)S(1)}, s32[1,16]{1,0:T(1,128)}, u32[]{:S(2)}) copy-start(s32[1,16]{1,0:T(1,128)} %param.15) | copy-start | bytes 196
  88.2 56.1 %all-to-all-start.1 = ((f32[16,128,256]{2,1,0:T(8,128)}), f32[16,128,256]{2,1,0:T(8,128)}, u32[]{:S(2)}, u32[]{:S(2)}) async-start(f32[16,128,256]{2,1,0:T(8,128)} %slice.15), calls=%async_computation.2 | async-start | bytes 4194304 | tf_op jit(solution)/shard_map/all_to_all | solution.py:37
  95.3 78.3 %all-gather.3.cloned.1.call-start = ((), (), s32[]{:S(2)}) async-start(), calls=%async_computation.6 | async-start | bytes 2228224 | tf_op jit(solution)/shard_map/all_gather | solution.py:47
  144.3 4.2 %copy-start.5 = (bf16[4,128,256]{2,1,0:T(8,128)(2,1)S(1)}, bf16[4,128,256]{2,1,0:T(8,128)(2,1)}, u32[]{:S(2)}) copy-start(bf16[4,128,256]{2,1,0:T(8,128)(2,1)} %copy-done.4) | copy-start | bytes 786436
Sparse Core Ops, SparseCore 0:
  60.9 8.6 reduce-scatter.2
  72.5 8.9 reduce-scatter.4
  98.8 74.7 all-gather.2
